TPU v7x, 32 devices: a 4x4x1 block of a 4x4x8 slice. The times are simulated.
32 devices in a mesh: data: 1 (over z), stage: 32 (over y, x, core).
Axes of the slice: x: 4, y: 4, z: 1, core: 2. Of those that a mesh axis runs over, the one named last changes fastest.
The devices are a block of a 4x4x8 slice.
Arguments:
- x_enc: bfloat16 [512, 256, 1024], P(('data', 'stage'))
- enc_len: int32 [512], P(('data', 'stage'))
- y: bfloat16 [512, 64, 1024], P(('data', 'stage'))
- enc_wqkv: bfloat16 [2, 1024, 3, 16, 128], replicated
- enc_wo: bfloat16 [2, 16, 128, 1024], replicated
- enc_w1: bfloat16 [2, 1024, 3072], replicated
- enc_w2: bfloat16 [2, 3072, 1024], replicated
- dec_wqkv: bfloat16 [2, 1024, 3, 16, 128], replicated
- dec_wo: bfloat16 [2, 16, 128, 1024], replicated
- cross_wq: bfloat16 [2, 1024, 8, 2, 128], replicated
- cross_wkv: bfloat16 [2, 1024, 2, 8, 128], replicated
- cross_wo: bfloat16 [2, 8, 2, 128, 1024], replicated
- dec_w1: bfloat16 [2, 1024, 3072], replicated
- dec_w2: bfloat16 [2, 3072, 1024], replicated
Outputs:
- output: bfloat16 [512, 64, 1024], P(('data', 'stage'))
All inputs are finite; a program needn't handle non-finite values.
Results may differ from a plain program's by a relative error of at most 0.0121753.
Values are sent between devices in bfloat16 or wider.
A program may use at most 768 MiB of HBM per device.

v0:
```python
import jax
import jax.numpy as jnp
from jax import lax
from jax.sharding import PartitionSpec as P, NamedSharding


def rms_norm(inputs):
    wide = inputs.astype(jnp.float32)
    return (wide * lax.rsqrt(jnp.mean(wide * wide, axis=-1, keepdims=True) + 1e-6)).astype(jnp.bfloat16)


def attend(query, keys, values, valid):
    scale = query.shape[-1] ** -0.5
    scores = jnp.einsum("bqgrd,bkgd->bgrqk", query, keys, preferred_element_type=jnp.float32) * scale
    attn_probs = jax.nn.softmax(jnp.where(valid, scores, -1e30), axis=-1).astype(jnp.bfloat16)
    return jnp.einsum("bgrqk,bkgd->bqgrd", attn_probs, values, preferred_element_type=jnp.float32).astype(jnp.bfloat16)


def self_block(state, w_qkv, w_out, valid):
    proj_qkv = jnp.einsum("bsd,dthe->tbshe", rms_norm(state), w_qkv, preferred_element_type=jnp.float32).astype(jnp.bfloat16)
    mixed = attend(proj_qkv[0][:, :, :, None, :], proj_qkv[1], proj_qkv[2], valid)
    update = jnp.einsum("bshre,hev->bsv", mixed, w_out, preferred_element_type=jnp.float32)
    return (state.astype(jnp.float32) + update).astype(jnp.bfloat16)


def ffn_block(state, w_in, w_out):
    hidden = jax.nn.gelu(jnp.einsum("bsd,df->bsf", rms_norm(state), w_in, preferred_element_type=jnp.float32)).astype(jnp.bfloat16)
    update = jnp.einsum("bsf,fd->bsd", hidden, w_out, preferred_element_type=jnp.float32)
    return (state.astype(jnp.float32) + update).astype(jnp.bfloat16)


def encoder(x_enc, enc_len, enc_wqkv, enc_wo, enc_w1, enc_w2):
    valid = (jnp.arange(x_enc.shape[1])[None, :] < enc_len[:, None])[:, None, None, None, :]
    state = x_enc
    for layer in range(enc_wqkv.shape[0]):
        state = self_block(state, enc_wqkv[layer], enc_wo[layer], valid)
        state = ffn_block(state, enc_w1[layer], enc_w2[layer])
    return rms_norm(state)


def decoder(y, kv_all, kv_len, dec_wqkv, dec_wo, cross_wq, cross_wo, dec_w1, dec_w2):
    positions = jnp.arange(y.shape[1])
    causal = positions[None, :] <= positions[:, None]
    keep = (jnp.arange(kv_all.shape[3])[None, :] < kv_len[:, None])[:, None, None, None, :]
    state = y
    for layer in range(dec_wqkv.shape[0]):
        state = self_block(state, dec_wqkv[layer], dec_wo[layer], causal)
        query = jnp.einsum("bsd,dgre->bsgre", rms_norm(state), cross_wq[layer], preferred_element_type=jnp.float32).astype(jnp.bfloat16)
        mixed = attend(query, kv_all[layer, 0], kv_all[layer, 1], keep)
        update = jnp.einsum("bsgre,grev->bsv", mixed, cross_wo[layer], preferred_element_type=jnp.float32)
        state = (state.astype(jnp.float32) + update).astype(jnp.bfloat16)
        state = ffn_block(state, dec_w1[layer], dec_w2[layer])
    return state


def solution(mesh):
    stages = mesh.shape["stage"]
    swap = [(source, (source + stages // 2) % stages) for source in range(stages)]
    rows = P(("data", "stage"))
    whole = P()

    def body(x_enc, enc_len, y, enc_wqkv, enc_wo, enc_w1, enc_w2, dec_wqkv, dec_wo, cross_wq, cross_wkv, cross_wo, dec_w1, dec_w2):
        enc_out = encoder(x_enc, enc_len, enc_wqkv, enc_wo, enc_w1, enc_w2)
        kv_all = jnp.einsum("bsd,ldtge->ltbsge", enc_out, cross_wkv, preferred_element_type=jnp.float32).astype(jnp.bfloat16)
        kv_recv = lax.ppermute(kv_all, "stage", swap)
        len_recv = lax.ppermute(enc_len, "stage", swap)
        return decoder(y, kv_recv, len_recv, dec_wqkv, dec_wo, cross_wq, cross_wo, dec_w1, dec_w2)

    return jax.shard_map(body, mesh=mesh, in_specs=(rows, rows, rows) + (whole,) * 11, out_specs=rows, check_vma=False)
```

profile of v0, /device:TPU:97, one launch (start us, length us, event | category | flops | bytes accessed | tf_op | source)
XLA Modules:
  0.0 1510.2 jit_solution(6598677627930265960)
XLA Ops:
  1.3 18.9 %fusion.387 = (bf16[1,1024,3,16,128]{4,3,2,1,0:T(8,128)(2,1)}, bf16[1,1024,3,16,128]{4,3,2,1,0:T(8,128)(2,1)}) fusion(bf16[2,1024,3,16,128]{4,3,2,1,0:T(8,128)(2,1)} %param.17), kind=kLoop, calls=%fused_computation.330 | loop fusion | bytes 50331648 | tf_op jit(solution)/shard_map/slice | solution.py:36
  22.0 62.5 %convert_bitcast_fusion.1 = bf16[3,16,256,16,128]{4,2,3,0,1:T(8,128)(2,1)} fusion(bf16[1,1024,3,16,128]{4,3,2,1,0:T(8,128)(2,1)} %get-tuple-element.8, bf16[16,256,1024]{2,1,0:T(8,128)(2,1)} %param.14, f32[16,256]{1,0:T(8,128)S(1)} %add_rsqrt_fusion.4), kind=kOutput, calls=%fused_computation.33 | convolution fusion | flops 51577356288 | bytes 71319552 | tf_op jit(solution)/shard_map/bsd,dthe->tbshe/dot_general | solution.py:20
  84.4 40.4 %bitcast_reduce_fusion.1 = (f32[16,16,256]{2,1,0:T(8,128)S(1)}, f32[16,16,256,256]{3,2,1,0:T(8,128)}) fusion(pred[16,256]{1,0:T(8,128)(4,1)S(1)} %copy-done.4, bf16[3,16,256,16,128]{4,2,3,0,1:T(8,128)(2,1)} %convert_bitcast_fusion.1), kind=kOutput, calls=%fused_computation.9 | convolution fusion | flops 4345233408 | bytes 100929536 | tf_op jit(solution)/shard_map/bqgrd,bkgd->bgrqk/dot_general | solution.py:14
  124.9 21.4 %fusion.4 = f32[16,16,256]{2,1,0:T(8,128)S(1)} fusion(f32[16,16,256,256]{3,2,1,0:T(8,128)} %get-tuple-element.14, f32[16,16,256]{2,1,0:T(8,128)S(1)} %get-tuple-element.13, pred[16,256]{1,0:T(8,128)(4,1)S(1)} %copy-done.4), kind=kLoop, calls=%fused_computation.14 | loop fusion | flops 67043328 | bytes 67637248 | tf_op jit(solution)/shard_map/reduce_sum | solution.py:15
  146.3 44.6 %fusion.33 = (f32[16,256]{1,0:T(8,128)S(1)}, bf16[16,256,1024]{2,1,0:T(8,128)(2,1)}) fusion(bf16[2,16,128,1024]{3,2,1,0:T(8,128)(2,1)} %param.18, f32[16,16,256]{2,1,0:T(8,128)S(1)} %fusion.4, f32[16,16,256]{2,1,0:T(8,128)S(1)} %get-tuple-element.13, f32[16,16,256,256]{3,2,1,0:T(8,128)} %get-tuple-element.14, pred[16,256]{1,0:T(8,128)(4,1)S(1)} %copy-done.4, ...), kind=kOutput, calls=%fused_computation.62 | convolution fusion | flops 21592272896 | bytes 105402368 | tf_op jit(solution)/shard_map/bshre,hev->bsv/dot_general | solution.py:22
  190.8 41.0 %fusion.13.clone.3.clone.5 = bf16[16,256,3072]{2,1,0:T(8,128)(2,1)} fusion(bf16[16,256,1024]{2,1,0:T(8,128)(2,1)} %get-tuple-element.16, f32[16,256]{1,0:T(8,128)S(1)} %add_rsqrt_fusion.3, bf16[2,1024,3072]{2,1,0:T(8,128)(2,1)} %param.19), kind=kOutput, calls=%fused_computation.23.clone.clone.clone.clone.clone.clone.clone.2 | convolution fusion | flops 25895632896 | bytes 39862272 | tf_op jit(solution)/shard_map/bsd,df->bsf/dot_general | solution.py:27
  231.8 33.4 %fusion.36 = (f32[16,256]{1,0:T(8,128)S(1)}, bf16[16,256,1024]{2,1,0:T(8,128)(2,1)}) fusion(bf16[2,3072,1024]{2,1,0:T(8,128)(2,1)} %param.20, bf16[16,256,1024]{2,1,0:T(8,128)(2,1)S(1)} %copy-done.9, bf16[16,256,3072]{2,1,0:T(8,128)(2,1)} %fusion.13.clone.3.clone.5), kind=kOutput, calls=%fused_computation.65 | convolution fusion | flops 25794965504 | bytes 48250880 | tf_op jit(solution)/shard_map/bsf,fd->bsd/dot_general | solution.py:28
  265.2 62.6 %convert_bitcast_fusion = bf16[3,16,256,16,128]{4,2,3,0,1:T(8,128)(2,1)} fusion(bf16[1,1024,3,16,128]{4,3,2,1,0:T(8,128)(2,1)} %get-tuple-element.7, bf16[16,256,1024]{2,1,0:T(8,128)(2,1)} %get-tuple-element.18, f32[16,256]{1,0:T(8,128)S(1)} %add_rsqrt_fusion.2), kind=kOutput, calls=%fused_computation.32 | convolution fusion | flops 51577356288 | bytes 71319552 | tf_op jit(solution)/shard_map/bsd,dthe->tbshe/dot_general | solution.py:20
  327.8 40.2 %bitcast_reduce_fusion = (f32[16,16,256]{2,1,0:T(8,128)S(1)}, f32[16,16,256,256]{3,2,1,0:T(8,128)}) fusion(pred[16,256]{1,0:T(8,128)(4,1)S(1)} %copy-done.5, bf16[3,16,256,16,128]{4,2,3,0,1:T(8,128)(2,1)} %convert_bitcast_fusion), kind=kOutput, calls=%fused_computation.5 | convolution fusion | flops 4345233408 | bytes 100929536 | tf_op jit(solution)/shard_map/bqgrd,bkgd->bgrqk/dot_general | solution.py:14
  368.0 21.6 %fusion.5 = f32[16,16,256]{2,1,0:T(8,128)S(1)} fusion(f32[16,16,256,256]{3,2,1,0:T(8,128)} %get-tuple-element.20, f32[16,16,256]{2,1,0:T(8,128)S(1)} %get-tuple-element.19, pred[16,256]{1,0:T(8,128)(4,1)S(1)} %copy-done.5), kind=kLoop, calls=%fused_computation.15 | loop fusion | flops 67043328 | bytes 67637248 | tf_op jit(solution)/shard_map/reduce_sum | solution.py:15
  389.6 44.6 %fusion.39 = (f32[16,256]{1,0:T(8,128)S(1)}, bf16[16,256,1024]{2,1,0:T(8,128)(2,1)}) fusion(bf16[2,16,128,1024]{3,2,1,0:T(8,128)(2,1)} %param.18, f32[16,16,256]{2,1,0:T(8,128)S(1)} %fusion.5, f32[16,16,256]{2,1,0:T(8,128)S(1)} %get-tuple-element.19, f32[16,16,256,256]{3,2,1,0:T(8,128)} %get-tuple-element.20, pred[16,256]{1,0:T(8,128)(4,1)S(1)} %copy-done.5, ...), kind=kOutput, calls=%fused_computation.68 | convolution fusion | flops 21592272896 | bytes 105402368 | tf_op jit(solution)/shard_map/bshre,hev->bsv/dot_general | solution.py:22
  434.2 40.6 %fusion.21.clone.3.clone.5 = bf16[16,256,3072]{2,1,0:T(8,128)(2,1)} fusion(bf16[16,256,1024]{2,1,0:T(8,128)(2,1)} %get-tuple-element.22, f32[16,256]{1,0:T(8,128)S(1)} %add_rsqrt_fusion.1, bf16[2,1024,3072]{2,1,0:T(8,128)(2,1)} %param.19), kind=kOutput, calls=%fused_computation.31.clone.clone.clone.clone.clone.clone.clone.2 | convolution fusion | flops 25895632896 | bytes 39862272 | tf_op jit(solution)/shard_map/bsd,df->bsf/dot_general | solution.py:27
  474.8 33.8 %fusion.28 = (f32[16,256]{1,0:T(8,128)S(1)}, bf16[16,256,1024]{2,1,0:T(8,128)(2,1)}) fusion(bf16[2,3072,1024]{2,1,0:T(8,128)(2,1)} %param.20, bf16[16,256,1024]{2,1,0:T(8,128)(2,1)S(1)} %copy-done.8, bf16[16,256,3072]{2,1,0:T(8,128)(2,1)} %fusion.21.clone.3.clone.5), kind=kOutput, calls=%fused_computation.57 | convolution fusion | flops 25794965504 | bytes 48250880 | tf_op jit(solution)/shard_map/bsf,fd->bsd/dot_general | solution.py:28
  508.6 43.2 %convert_bitcast_fusion.2 = bf16[2,2,16,256,8,128]{5,3,4,1,0,2:T(8,128)(2,1)} fusion(bf16[16,256,1024]{2,1,0:T(8,128)(2,1)} %get-tuple-element.24, bf16[2,1024,2,8,128]{4,3,2,1,0:T(8,128)(2,1)} %param.24, f32[16,256]{1,0:T(8,128)S(1)} %add_rsqrt_fusion), kind=kOutput, calls=%fused_computation.38 | convolution fusion | flops 34389098496 | bytes 50348032 | tf_op jit(solution)/shard_map/bsd,ldtge->ltbsge/dot_general | solution.py:64
  557.4 18.6 %fusion.386 = (bf16[1,1024,3,16,128]{4,3,2,1,0:T(8,128)(2,1)}, bf16[1,1024,3,16,128]{4,3,2,1,0:T(8,128)(2,1)}) fusion(bf16[2,1024,3,16,128]{4,3,2,1,0:T(8,128)(2,1)} %param.21), kind=kLoop, calls=%fused_computation.329 | loop fusion | bytes 50331648 | tf_op jit(solution)/shard_map/slice | solution.py:47
  576.0 20.8 %convert_bitcast_fusion.4 = bf16[3,16,64,16,128]{4,2,3,0,1:T(8,128)(2,1)} fusion(bf16[1,1024,3,16,128]{4,3,2,1,0:T(8,128)(2,1)} %get-tuple-element.6, bf16[16,64,1024]{2,1,0:T(8,128)(2,1)S(1)} %copy-done.3, f32[16,64]{1,0:T(8,128)S(1)} %add_rsqrt_fusion.10), kind=kOutput, calls=%fused_computation.120 | convolution fusion | flops 12894339072 | bytes 27267072 | tf_op jit(solution)/shard_map/bsd,dthe->tbshe/dot_general | solution.py:20
  630.0 646.4 %collective-permute-done.1 = s32[16]{0:T(128)S(1)} collective-permute-done((s32[16]{0:T(128)S(1)}, s32[16]{0:T(128)S(1)}, u32[]{:S(2)}, u32[]{:S(2)}) %collective-permute-start.1) | collective-permute-done | bytes 96 | tf_op jit(solution)/shard_map/ppermute | solution.py:66
  1290.1 17.3 %fusion.402 = f32[16,8,2,64]{3,2,1,0:T(2,128)S(1)} fusion(f32[16,8,256,64,2]{2,3,4,1,0:T(8,128)} %fusion.98, pred[16,256]{1,0:T(8,128)(4,1)S(1)} %iota_compare_fusion.1), kind=kOutput, calls=%fused_computation.331 | output fusion | flops 25166080 | bytes 16846848 | tf_op jit(solution)/shard_map/sub | solution.py:15
  1307.4 41.9 %fusion.173 = (f32[16,64]{1,0:T(8,128)S(1)}, bf16[16,64,1024]{2,1,0:T(8,128)(2,1)}) fusion(bf16[2,8,2,128,1024]{4,3,2,1,0:T(8,128)(2,1)} %param.25, f32[16,8,2,64]{3,2,1,0:T(2,128)S(1)} %fusion.402, bf16[2,2,16,256,8,128]{5,3,4,1,0,2:T(8,128)(2,1)} %collective-permute-done, f32[16,8,256,64,2]{2,3,4,1,0:T(8,128)} %fusion.98, ...), kind=kOutput, calls=%fused_computation.207 | convolution fusion | flops 5406473216 | bytes 50475008 | tf_op jit(solution)/shard_map/bsgre,grev->bsv/dot_general | solution.py:50
  1349.4 20.4 %fusion.176 = (f32[16,64]{1,0:T(8,128)S(1)}, bf16[16,64,1024]{2,1,0:T(8,128)(2,1)}) fusion(bf16[2,3072,1024]{2,1,0:T(8,128)(2,1)} %param.27, bf16[2,1024,3072]{2,1,0:T(8,128)(2,1)} %param.26, bf16[16,64,1024]{2,1,0:T(8,128)(2,1)} %get-tuple-element.28, f32[16,64]{1,0:T(8,128)S(1)} %add_rsqrt_fusion.8), kind=kOutput, calls=%fused_computation.210 | convolution fusion | flops 12922649600 | bytes 18882560 | tf_op jit(solution)/shard_map/bsf,fd->bsd/dot_general | solution.py:28
  1369.8 21.7 %convert_bitcast_fusion.3 = bf16[3,16,64,16,128]{4,2,3,0,1:T(8,128)(2,1)} fusion(bf16[1,1024,3,16,128]{4,3,2,1,0:T(8,128)(2,1)} %get-tuple-element.5, bf16[16,64,1024]{2,1,0:T(8,128)(2,1)} %get-tuple-element.30, f32[16,64]{1,0:T(8,128)S(1)} %add_rsqrt_fusion.7), kind=kOutput, calls=%fused_computation.119 | convolution fusion | flops 12894339072 | bytes 27267072 | tf_op jit(solution)/shard_map/bsd,dthe->tbshe/dot_general | solution.py:20
  1430.1 17.3 %fusion.411 = f32[16,8,2,64]{3,2,1,0:T(2,128)S(1)} fusion(f32[16,8,256,64,2]{2,3,4,1,0:T(8,128)} %fusion.96, pred[16,256]{1,0:T(8,128)(4,1)S(1)} %iota_compare_fusion.1), kind=kOutput, calls=%fused_computation.332 | output fusion | flops 25166080 | bytes 16846848 | tf_op jit(solution)/shard_map/sub | solution.py:15
  1447.4 42.0 %fusion.182 = (f32[16,64]{1,0:T(8,128)S(1)}, bf16[16,64,1024]{2,1,0:T(8,128)(2,1)}) fusion(bf16[2,8,2,128,1024]{4,3,2,1,0:T(8,128)(2,1)} %param.25, f32[16,8,2,64]{3,2,1,0:T(2,128)S(1)} %fusion.411, bf16[2,2,16,256,8,128]{5,3,4,1,0,2:T(8,128)(2,1)} %collective-permute-done, f32[16,8,256,64,2]{2,3,4,1,0:T(8,128)} %fusion.96, ...), kind=kOutput, calls=%fused_computation.216 | convolution fusion | flops 5406473216 | bytes 50475008 | tf_op jit(solution)/shard_map/bsgre,grev->bsv/dot_general | solution.py:50
  1489.4 20.5 %fusion.184 = bf16[16,64,1024]{2,1,0:T(8,128)(2,1)} fusion(bf16[16,64,1024]{2,1,0:T(8,128)(2,1)} %get-tuple-element.36, bf16[2,3072,1024]{2,1,0:T(8,128)(2,1)} %param.27, bf16[2,1024,3072]{2,1,0:T(8,128)(2,1)} %param.26, f32[16,64]{1,0:T(8,128)S(1)} %add_rsqrt_fusion.5), kind=kOutput, calls=%fused_computation.218 | convolution fusion | flops 12919504896 | bytes 18878464 | tf_op jit(solution)/shard_map/bsf,fd->bsd/dot_general | solution.py:28
  (48 shorter events, 94.2 us)
Async XLA Ops:
  1.3 18.9 %copy-start.2 = (bf16[16,256,1024]{2,1,0:T(8,128)(2,1)S(1)}, bf16[16,256,1024]{2,1,0:T(8,128)(2,1)}, u32[]{:S(2)}) copy-start(bf16[16,256,1024]{2,1,0:T(8,128)(2,1)} %param.14) | copy-start | bytes 25165828
  22.0 62.5 %copy-start.4 = (pred[16,256]{1,0:T(8,128)(4,1)S(1)}, pred[16,256]{1,0:T(8,128)(4,1)}, u32[]{:S(2)}) copy-start(pred[16,256]{1,0:T(8,128)(4,1)} %iota_compare_fusion.2) | copy-start | bytes 12292
  190.8 41.0 %copy-start.9 = (bf16[16,256,1024]{2,1,0:T(8,128)(2,1)S(1)}, bf16[16,256,1024]{2,1,0:T(8,128)(2,1)}, u32[]{:S(2)}) copy-start(bf16[16,256,1024]{2,1,0:T(8,128)(2,1)} %get-tuple-element.16) | copy-start | bytes 25165828
  265.2 62.6 %copy-start.5 = (pred[16,256]{1,0:T(8,128)(4,1)S(1)}, pred[16,256]{1,0:T(8,128)(4,1)}, u32[]{:S(2)}) copy-start(pred[16,256]{1,0:T(8,128)(4,1)} %iota_compare_fusion.2) | copy-start | bytes 12292
  434.2 40.6 %copy-start.8 = (bf16[16,256,1024]{2,1,0:T(8,128)(2,1)S(1)}, bf16[16,256,1024]{2,1,0:T(8,128)(2,1)}, u32[]{:S(2)}) copy-start(bf16[16,256,1024]{2,1,0:T(8,128)(2,1)} %get-tuple-element.22) | copy-start | bytes 25165828
  508.6 48.1 %copy-start.6 = (s32[16]{0:T(128)S(1)}, s32[16]{0:T(128)}, u32[]{:S(2)}) copy-start(s32[16]{0:T(128)} %param.15) | copy-start | bytes 196
  508.6 48.3 %copy-start.3 = (bf16[16,64,1024]{2,1,0:T(8,128)(2,1)S(1)}, bf16[16,64,1024]{2,1,0:T(8,128)(2,1)}, u32[]{:S(2)}) copy-start(bf16[16,64,1024]{2,1,0:T(8,128)(2,1)} %param.16) | copy-start | bytes 6291460
  551.8 724.7 %collective-permute-start = (bf16[2,2,16,256,8,128]{5,3,4,1,0,2:T(8,128)(2,1)}, bf16[2,2,16,256,8,128]{5,3,4,1,0,2:T(8,128)(2,1)}, u32[]{:S(2)}, u32[]{:S(2)}) collective-permute-start(bf16[2,2,16,256,8,128]{5,3,4,1,0,2:T(8,128)(2,1)} %convert_bitcast_fusion.2), channel_id=1, source_target_pairs={{0,16},{1,17},{2,18},{3,19},{4,20},{5,21},{6,22},{7,23},{8,24},{9,... | collective-permute-start | bytes 100663304 | tf_op jit(solution)/shard_map/ppermute | solution.py:65
  556.7 719.7 %collective-permute-start.1 = (s32[16]{0:T(128)S(1)}, s32[16]{0:T(128)S(1)}, u32[]{:S(2)}, u32[]{:S(2)}) collective-permute-start(s32[16]{0:T(128)S(1)} %copy-done.6), channel_id=1, source_target_pairs={{0,16},{1,17},{2,18},{3,19},{4,20},{5,21},{6,22},{7,23},{8,24},{9,... | collective-permute-start | bytes 200 | tf_op jit(solution)/shard_map/ppermute | solution.py:66
  602.6 3.3 copy-start
  1397.3 3.3 copy-start.1
  1430.1 17.3 %copy-start.7 = (bf16[16,64,1024]{2,1,0:T(8,128)(2,1)S(1)}, bf16[16,64,1024]{2,1,0:T(8,128)(2,1)}, u32[]{:S(2)}) copy-start(bf16[16,64,1024]{2,1,0:T(8,128)(2,1)} %get-tuple-element.34) | copy-start | bytes 6291460
where the time goes:
time: 1520 us; the launch traced here: 1510 us
  matrix products  718 us (47%)
  waiting for transfers between devices  646 us (42%)
  other arithmetic  87.1 us (6%)
  local copies, waits for them, and re-layouts  52.6 us (3%)
    ppermute x1, waiting for transfers between devices, body(): len_recv = lax.ppermute(enc_len, 'stage', swap)  646 us
    dot_general x4, matrix products, self_block(): jnp.einsum('bsd,dthe->tbshe', rms_norm(state), w_qkv, preferred_element_t...  168 us
    dot_general x6, matrix products, attend(): jnp.einsum('bqgrd,bkgd->bgrqk', query, keys, preferred_element_type=jnp.f...  120 us
    dot_general x4, matrix products, self_block(): jnp.einsum('bshre,hev->bsv', mixed, w_out, preferred_element_type=jnp.flo...  115 us
    dot_general x4, matrix products, ffn_block(): jnp.einsum('bsf,fd->bsd', hidden, w_out, preferred_element_type=jnp.float32)  108 us
    dot_general x2, matrix products, decoder(): jnp.einsum('bsgre,grev->bsv', mixed, cross_wo[layer], preferred_element_t...  83.9 us
    dot_general x2, matrix products, ffn_block(): jnp.einsum('bsd,df->bsf', rms_norm(state), w_in, preferred_element_type=j...  81.5 us
    reduce_sum x4, other arithmetic, attend(): jax.nn.softmax(jnp.where(valid, scores, -1e+30), axis=-1)  48.9 us
  transfers between devices with their start and end apart: 2, of which 1 were waited for; matrix products, arithmetic and copies ran while one was open for 5% of the time, Pallas kernels for 0%

commit v1 on v0

v1 whole, which is shorter than its diff:
```python
import functools
import math

import jax
import jax.numpy as jnp
from jax import lax
from jax.experimental import pallas as pl
from jax.experimental.pallas import tpu as pltpu
from jax.sharding import PartitionSpec as P

NEG = -1e30
VMEM_LIMIT = 60 * 1024 * 1024
ENC_STEP = 2
DEC_STEP = 4


def rms_norm(inputs):
    wide = inputs.astype(jnp.float32)
    return (wide * lax.rsqrt(jnp.mean(wide * wide, axis=-1, keepdims=True) + 1e-6)).astype(jnp.bfloat16)


def dot(left, right):
    return jnp.dot(left, right, preferred_element_type=jnp.float32)


def attend(query, keys, values, valid):
    scores = lax.dot_general(query, keys, (((1,), (1,)), ((), ())), preferred_element_type=jnp.float32)
    scores = jnp.where(valid, scores, NEG)
    top = jnp.max(scores, axis=-1, keepdims=True)
    weights = jnp.exp2((scores - top) * (query.shape[-1] ** -0.5 * math.log2(math.e)))
    probs = (weights * (1.0 / jnp.sum(weights, axis=-1, keepdims=True))).astype(jnp.bfloat16)
    return dot(probs, values).astype(jnp.bfloat16)


def gelu(x):
    half = 0.5 * x
    root = math.sqrt(2.0 / math.pi)
    return (half + half * jnp.tanh(x * (root + (root * 0.044715) * (x * x)))).astype(jnp.bfloat16)


def ffn(state, w1, w2, hidden, chunk):
    normed = rms_norm(state)
    width = w1.shape[1]
    for start in range(0, width, chunk):
        cols = pl.ds(start, chunk)
        hidden[:, cols] = gelu(dot(normed, w1[:, cols]))
    return (state.astype(jnp.float32) + dot(hidden[...], w2[...])).astype(jnp.bfloat16)


def weight_copies(layer, sources, targets, sems):
    return [
        pltpu.make_async_copy(source.at[layer], target, sems.at[i])
        for i, (source, target) in enumerate(zip(sources, targets))
    ]


def enc_kernel(layer, chunk, len_ref, qkv_ref, x_ref, wo_hbm, w1_hbm, w2_hbm, out_ref, wo, w1, w2, mixed, state_s, hidden, sems):
    step = pl.program_id(0)
    first = step == 0
    copies = weight_copies(layer, (wo_hbm, w1_hbm, w2_hbm), (wo, w1, w2), sems)

    @pl.when(first)
    def _():
        for copy in copies:
            copy.start()

    seqs, _, heads, length, head = qkv_ref.shape

    def one(b, carry):
        rows = pl.ds(pl.multiple_of(b * length, length), length)
        valid = lax.broadcasted_iota(jnp.int32, (1, length), 1) < len_ref[step * seqs + b]
        for h in range(heads):
            mixed[rows, h * head:(h + 1) * head] = attend(qkv_ref[b, 0, h], qkv_ref[b, 1, h], qkv_ref[b, 2, h], valid)
        return carry

    lax.fori_loop(0, seqs, one, 0)

    @pl.when(first)
    def _():
        copies[0].wait()

    x = x_ref[...].reshape(seqs * length, x_ref.shape[-1])
    state_s[...] = (x.astype(jnp.float32) + dot(mixed[...], wo[...])).astype(jnp.bfloat16)

    @pl.when(first)
    def _():
        copies[1].wait()
        copies[2].wait()

    out_ref[...] = ffn(state_s[...], w1, w2, hidden, chunk).reshape(out_ref.shape)


def dec_kernel(layer, chunk, len_ref, qkv_ref, y_ref, kv_ref, wo_hbm, wq_hbm, cwo_hbm, w1_hbm, w2_hbm, out_ref,
               wo, wq, cwo, w1, w2, mixed, query_s, state_s, hidden, sems):
    step = pl.program_id(0)
    first = step == 0
    copies = weight_copies(layer, (wo_hbm, wq_hbm, cwo_hbm, w1_hbm, w2_hbm), (wo, wq, cwo, w1, w2), sems)

    @pl.when(first)
    def _():
        for copy in copies:
            copy.start()

    seqs, _, heads, length, head = qkv_ref.shape
    rows = seqs * length
    groups, keys_len = kv_ref.shape[3], kv_ref.shape[4]
    rep = heads // groups
    row = lax.broadcasted_iota(jnp.int32, (rows, rows), 0)
    col = lax.broadcasted_iota(jnp.int32, (rows, rows), 1)
    causal = (col <= row) & (col >= row - lax.rem(row, length))
    for h in range(heads):
        query, keys, values = (qkv_ref[:, t, h].reshape(rows, head) for t in range(3))
        mixed[:, h * head:(h + 1) * head] = attend(query, keys, values, causal)

    @pl.when(first)
    def _():
        copies[0].wait()
        copies[1].wait()

    y = y_ref[...].reshape(rows, y_ref.shape[-1])
    state_s[...] = (y.astype(jnp.float32) + dot(mixed[...], wo[...])).astype(jnp.bfloat16)
    query_s[...] = dot(rms_norm(state_s[...]), wq[...]).astype(jnp.bfloat16)

    for b in range(seqs):
        valid = lax.broadcasted_iota(jnp.int32, (1, keys_len), 1) < len_ref[step * seqs + b]
        at = slice(b * length, (b + 1) * length)
        for g in range(groups):
            spans = [slice((g * rep + r) * head, (g * rep + r + 1) * head) for r in range(rep)]
            query = jnp.concatenate([query_s[at, span] for span in spans], axis=0)
            result = attend(query, kv_ref[0, b, 0, g], kv_ref[0, b, 1, g], valid)
            for r, span in enumerate(spans):
                mixed[at, span] = result[r * length:(r + 1) * length]

    @pl.when(first)
    def _():
        for copy in copies[2:]:
            copy.wait()

    state_s[...] = (state_s[...].astype(jnp.float32) + dot(mixed[...], cwo[...])).astype(jnp.bfloat16)
    out_ref[...] = ffn(state_s[...], w1, w2, hidden, chunk).reshape(out_ref.shape)


def call(kernel, step_seqs, lens, qkv, state, others, weights, layer, flops):
    n_seq, _, heads, length, head = qkv.shape
    d = state.shape[-1]
    width = weights[-1].shape[1]
    seqs = math.gcd(step_seqs, n_seq)
    rows = seqs * length
    block = lambda *tail: pl.BlockSpec((seqs,) + tail, lambda i, lens: (i,) + (0,) * len(tail))
    scratch = [pltpu.VMEM(w.shape[1:], w.dtype) for w in weights]
    scratch.append(pltpu.VMEM((rows, heads * head), jnp.bfloat16))
    if others:
        scratch.append(pltpu.VMEM((rows, heads * head), jnp.bfloat16))
    scratch += [pltpu.VMEM((rows, d), jnp.bfloat16), pltpu.VMEM((rows, width), jnp.bfloat16)]
    scratch.append(pltpu.SemaphoreType.DMA((len(weights),)))
    other_specs = [
        pl.BlockSpec((1, seqs) + o.shape[2:], lambda i, lens: (layer, i, 0, 0, 0, 0)) for o in others
    ]
    moved = 2 * sum(a.size for a in (qkv, state, state)) + sum(2 * w.size // w.shape[0] for w in weights)
    return pl.pallas_call(
        functools.partial(kernel, layer, min(width, 1024)),
        out_shape=jax.ShapeDtypeStruct(state.shape, state.dtype),
        grid_spec=pltpu.PrefetchScalarGridSpec(
            num_scalar_prefetch=1,
            grid=(n_seq // seqs,),
            in_specs=[block(3, heads, length, head), block(length, d)] + other_specs
            + [pl.BlockSpec(memory_space=pl.ANY)] * len(weights),
            out_specs=block(length, d),
            scratch_shapes=scratch,
        ),
        compiler_params=pltpu.CompilerParams(dimension_semantics=("arbitrary",), vmem_limit_bytes=VMEM_LIMIT),
        cost_estimate=pl.CostEstimate(flops=flops, bytes_accessed=moved, transcendentals=0),
    )(lens, qkv, state, *others, *weights)


def project_qkv(state, w_qkv):
    return jnp.einsum("bsd,dthe->bthse", rms_norm(state), w_qkv, preferred_element_type=jnp.float32).astype(jnp.bfloat16)


def merge_heads(w):
    return w.reshape(w.shape[0], -1, w.shape[-1])


def solution(mesh):
    stages = mesh.shape["stage"]
    swap = [(source, (source + stages // 2) % stages) for source in range(stages)]
    rows = P(("data", "stage"))
    whole = P()

    def body(x_enc, enc_len, y, enc_wqkv, enc_wo, enc_w1, enc_w2, dec_wqkv, dec_wo, cross_wq, cross_wkv, cross_wo, dec_w1, dec_w2):
        guest = lax.ppermute(y, "stage", swap)
        d = x_enc.shape[-1]
        enc_weights = [merge_heads(enc_wo), enc_w1, enc_w2]
        dec_weights = [merge_heads(dec_wo), cross_wq.reshape(cross_wq.shape[0], d, -1), merge_heads(cross_wo), dec_w1, dec_w2]
        macs = lambda ws: sum(w.size // w.shape[0] for w in ws)
        state = x_enc
        for layer in range(enc_wqkv.shape[0]):
            qkv = project_qkv(state, enc_wqkv[layer])
            flops = 2 * state.size // d * (macs(enc_weights) + 2 * qkv.shape[2] * qkv.shape[4] * x_enc.shape[1])
            state = call(enc_kernel, ENC_STEP, enc_len, qkv, state, [], enc_weights, layer, flops)
        kv_all = jnp.einsum("bsd,ldtge->lbtgse", rms_norm(state), cross_wkv, preferred_element_type=jnp.float32).astype(jnp.bfloat16)
        state = guest
        for layer in range(dec_wqkv.shape[0]):
            qkv = project_qkv(state, dec_wqkv[layer])
            flops = 2 * state.size // d * (macs(dec_weights) + 4 * qkv.shape[2] * qkv.shape[4] * x_enc.shape[1])
            state = call(dec_kernel, DEC_STEP, enc_len, qkv, state, [kv_all], dec_weights, layer, flops)
        return lax.ppermute(state, "stage", swap)

    return jax.shard_map(body, mesh=mesh, in_specs=(rows, rows, rows) + (whole,) * 11, out_specs=rows, check_vma=False)
```

time: 1520 us -> 702 us (0.46)
  waiting for transfers between devices: 646 us -> 47.3 us
  matrix products: 718 us -> 211 us
  Pallas kernels: 0 us -> 360 us
  other arithmetic: 87.1 us -> 16.1 us
    ppermute x2, waiting for transfers between devices: 646 us -> 47.3 us  [the longest x1 47.3 us: body(): return lax.ppermute(state, 'stage', swap)]
    dot_general x23 -> x5, matrix products: 718 us -> 211 us  [the longest x4 168 us: project_qkv(): jnp.einsum('bsd,dthe->bthse', rms_norm(state), w_qkv, preferred_element_t...]
    pallas_call x0 -> x4, Pallas kernels: none -> 360 us  [call(): pl.pallas_call(functools.partial(kernel, layer, min(width, 1024)), out_sh...]
    reduce_sum x4 -> x0, other arithmetic: 48.9 us -> none  [attend(): jax.nn.softmax(jnp.where(valid, scores, -1e+30), axis=-1)]
    sub x2 -> x0, other arithmetic: 34.6 us -> none  [attend(): jax.nn.softmax(jnp.where(valid, scores, -1e+30), axis=-1)]
  transfers between devices with their start and end apart: 2 -> 2, of which waited for: 1 -> 1; matrix products, arithmetic and copies ran while one was open for 5% -> 33% of each run, Pallas kernels for 0% -> 35%
where the time goes in v1:
time: 702 us; the launch traced here: 693 us
  Pallas kernels  360 us (51%)
  matrix products  211 us (30%)
  local copies, waits for them, and re-layouts  52.7 us (8%)
  waiting for transfers between devices  47.3 us (7%)
  other arithmetic  16.1 us (2%)
    pallas_call x4, Pallas kernels, call(): pl.pallas_call(functools.partial(kernel, layer, min(width, 1024)), out_sh...  360 us
    dot_general x4, matrix products, project_qkv(): jnp.einsum('bsd,dthe->bthse', rms_norm(state), w_qkv, preferred_element_t...  168 us
    ppermute x1, waiting for transfers between devices, body(): return lax.ppermute(state, 'stage', swap)  47.3 us
    dot_general x1, matrix products, body(): jnp.einsum('bsd,ldtge->lbtgse', rms_norm(state), cross_wkv, preferred_ele...  43 us
    slice x1, local copies, waits for them, and re-layouts, body(): qkv = project_qkv(state, enc_wqkv[layer])  18.5 us
    slice x1, local copies, waits for them, and re-layouts, body(): qkv = project_qkv(state, dec_wqkv[layer])  18.4 us
    reduce_sum x5, other arithmetic, rms_norm(): jnp.mean(wide * wide, axis=-1, keepdims=True) + 1e-06  16 us
    reshape x1, local copies, waits for them, and re-layouts, body(): cross_wq.reshape(cross_wq.shape[0], d, -1)  14.4 us
  transfers between devices with their start and end apart: 2, of which 1 were waited for; matrix products, arithmetic and copies ran while one was open for 33% of the time, Pallas kernels for 35%

profile of v1, /device:TPU:97, one launch (start us, length us, event | category | flops | bytes accessed | tf_op | source)
XLA Modules:
  0.0 692.6 jit_solution(16392675566342856943)
XLA Ops:
  0.0 0.0 copy-start
  0.0 4.8 collective-permute-start
  4.8 18.5 %fusion.28 = (bf16[1,1024,3,16,128]{4,3,2,1,0:T(8,128)(2,1)}, bf16[1,1024,3,16,128]{4,3,2,1,0:T(8,128)(2,1)}) fusion(bf16[2,1024,3,16,128]{4,3,2,1,0:T(8,128)(2,1)} %param.17), kind=kLoop, calls=%fused_computation.47 | loop fusion | bytes 50331648 | tf_op jit(solution)/shard_map/slice | solution.py:198
  23.4 0.0 copy-done
  23.4 1.7 fusion
  25.1 62.5 %convert_bitcast_fusion.1.qkv_ref = bf16[16,3,16,256,128]{4,3,2,1,0:T(8,128)(2,1)} fusion(bf16[1,1024,3,16,128]{4,3,2,1,0:T(8,128)(2,1)} %get-tuple-element.5, bf16[16,256,1024]{2,1,0:T(8,128)(2,1)} %x_ref.1, f32[16,256]{1,0:T(8,128)S(1)} %add_rsqrt_fusion.2), kind=kOutput, calls=%fused_computation.1 | convolution fusion | flops 51577356288 | bytes 71319552 | tf_op jit(solution)/shard_map/bsd,dthe->bthse/dot_general | solution.py:177
  87.6 122.6 %shard_map.136.x_ref = bf16[16,256,1024]{2,1,0:T(8,128)(2,1)} custom-call(s32[16]{0:T(128)} %len_ref.7, bf16[16,3,16,256,128]{4,3,2,1,0:T(8,128)(2,1)} %convert_bitcast_fusion.1.qkv_ref, bf16[16,256,1024]{2,1,0:T(8,128)(2,1)} %x_ref.1, bf16[2,2048,1024]{2,1,0:T(8,128)(2,1)} %bitcast.66, bf16[2,1024,3072]{2,1,0:T(8,128)(2,1)} %w1_hbm.5, ...), custom_call_target="tpu_custom_call" | custom-call | flops 77309411328 | bytes 83886080 | tf_op jit(solution)/shard_map/pallas_call | solution.py:160
  210.2 5.1 fusion.2
  215.3 62.7 %convert_bitcast_fusion.qkv_ref = bf16[16,3,16,256,128]{4,3,2,1,0:T(8,128)(2,1)} fusion(bf16[1,1024,3,16,128]{4,3,2,1,0:T(8,128)(2,1)} %get-tuple-element.6, bf16[16,256,1024]{2,1,0:T(8,128)(2,1)} %shard_map.136.x_ref, f32[16,256]{1,0:T(8,128)S(1)} %add_rsqrt_fusion.1), kind=kOutput, calls=%fused_computation | convolution fusion | flops 51577356288 | bytes 71319552 | tf_op jit(solution)/shard_map/bsd,dthe->bthse/dot_general | solution.py:177
  278.0 122.9 %shard_map.137 = bf16[16,256,1024]{2,1,0:T(8,128)(2,1)} custom-call(s32[16]{0:T(128)} %len_ref.7, bf16[16,3,16,256,128]{4,3,2,1,0:T(8,128)(2,1)} %convert_bitcast_fusion.qkv_ref, bf16[16,256,1024]{2,1,0:T(8,128)(2,1)} %shard_map.136.x_ref, bf16[2,2048,1024]{2,1,0:T(8,128)(2,1)} %bitcast.67, bf16[2,1024,3072]{2,1,0:T(8,128)(2,1)} %w1_hbm.5, ...), custom_call_target="tpu_custom_call" | custom-call | flops 77309411328 | bytes 83886080 | tf_op jit(solution)/shard_map/pallas_call | solution.py:160
  400.9 5.1 fusion.4
  406.0 43.0 %convert_bitcast_fusion.2.kv_ref = bf16[2,16,2,8,256,128]{5,4,3,2,1,0:T(8,128)(2,1)} fusion(bf16[16,256,1024]{2,1,0:T(8,128)(2,1)} %shard_map.137, bf16[2,1024,2,8,128,1]{4,3,2,1,0,5:T(8,128)(2,1)} %bitcast.68, f32[16,256]{1,0:T(8,128)S(1)} %add_rsqrt_fusion), kind=kOutput, calls=%fused_computation.2 | convolution fusion | flops 34389098496 | bytes 50348032 | tf_op jit(solution)/shard_map/bsd,ldtge->lbtgse/dot_general | solution.py:201
  449.0 14.4 %reshape.54.wq_hbm = bf16[2,1024,2048]{2,1,0:T(8,128)(2,1)} reshape(bf16[2,1024,8,2,128]{4,3,2,1,0:T(2,128)(2,1)} %param.23) | data formatting | bytes 16777216 | tf_op jit(solution)/shard_map/reshape | solution.py:194
  463.4 18.4 %fusion.29 = (bf16[1,1024,3,16,128]{4,3,2,1,0:T(8,128)(2,1)}, bf16[1,1024,3,16,128]{4,3,2,1,0:T(8,128)(2,1)}) fusion(bf16[2,1024,3,16,128]{4,3,2,1,0:T(8,128)(2,1)} %param.21), kind=kLoop, calls=%fused_computation.48 | loop fusion | bytes 50331648 | tf_op jit(solution)/shard_map/slice | solution.py:204
  481.8 0.0 collective-permute-done.y_ref
  481.8 2.1 fusion.18
  483.9 21.2 %convert_bitcast_fusion.4.qkv_ref = bf16[16,3,16,64,128]{4,3,2,1,0:T(8,128)(2,1)} fusion(bf16[1,1024,3,16,128]{4,3,2,1,0:T(8,128)(2,1)} %get-tuple-element.7, bf16[16,64,1024]{2,1,0:T(8,128)(2,1)} %collective-permute-done.y_ref, f32[16,64]{1,0:T(8,128)S(1)} %add_rsqrt_fusion.4), kind=kOutput, calls=%fused_computation.22 | convolution fusion | flops 12894339072 | bytes 27267072 | tf_op jit(solution)/shard_map/bsd,dthe->bthse/dot_general | solution.py:177
  505.1 57.5 %shard_map.138.y_ref = bf16[16,64,1024]{2,1,0:T(8,128)(2,1)} custom-call(s32[16]{0:T(128)} %len_ref.7, bf16[16,3,16,64,128]{4,3,2,1,0:T(8,128)(2,1)} %convert_bitcast_fusion.4.qkv_ref, bf16[16,64,1024]{2,1,0:T(8,128)(2,1)} %collective-permute-done.y_ref, bf16[2,16,2,8,256,128]{5,4,3,2,1,0:T(8,128)(2,1)} %convert_bitcast_fusion.2.kv_ref, ...), custom_call_target="tpu_custom_call" | custom-call | flops 30064771072 | bytes 41943040 | tf_op jit(solution)/shard_map/pallas_call | solution.py:160
  562.6 2.1 fusion.20
  564.7 21.4 %convert_bitcast_fusion.3.qkv_ref = bf16[16,3,16,64,128]{4,3,2,1,0:T(8,128)(2,1)} fusion(bf16[1,1024,3,16,128]{4,3,2,1,0:T(8,128)(2,1)} %get-tuple-element.8, bf16[16,64,1024]{2,1,0:T(8,128)(2,1)} %shard_map.138.y_ref, f32[16,64]{1,0:T(8,128)S(1)} %add_rsqrt_fusion.3), kind=kOutput, calls=%fused_computation.21 | convolution fusion | flops 12894339072 | bytes 27267072 | tf_op jit(solution)/shard_map/bsd,dthe->bthse/dot_general | solution.py:177
  586.1 57.0 %shard_map.139 = bf16[16,64,1024]{2,1,0:T(8,128)(2,1)} custom-call(s32[16]{0:T(128)} %len_ref.7, bf16[16,3,16,64,128]{4,3,2,1,0:T(8,128)(2,1)} %convert_bitcast_fusion.3.qkv_ref, bf16[16,64,1024]{2,1,0:T(8,128)(2,1)} %shard_map.138.y_ref, bf16[2,16,2,8,256,128]{5,4,3,2,1,0:T(8,128)(2,1)} %convert_bitcast_fusion.2.kv_ref, bf16[2,2048,1024]{2,1,0:T(8,128)(2,1)} %bitcast.70, ...), custom_call_target="tpu_custom_call" | custom-call | flops 30064771072 | bytes 41943040 | tf_op jit(solution)/shard_map/pallas_call | solution.py:160
  643.1 0.6 collective-permute-start.1
  643.7 47.3 %collective-permute-done.1 = bf16[16,64,1024]{2,1,0:T(8,128)(2,1)S(1)} collective-permute-done((bf16[16,64,1024]{2,1,0:T(8,128)(2,1)}, bf16[16,64,1024]{2,1,0:T(8,128)(2,1)S(1)}, u32[]{:S(2)}, u32[]{:S(2)}) %collective-permute-start.1) | collective-permute-done | bytes 2097184 | tf_op jit(solution)/shard_map/ppermute | solution.py:207
  691.0 1.3 copy.51
  (5 shorter events, 0.0 us)
Async XLA Ops:
  0.0 23.4 %copy-start = (bf16[16,256,1024]{2,1,0:T(8,128)(2,1)S(1)}, bf16[16,256,1024]{2,1,0:T(8,128)(2,1)}, u32[]{:S(2)}) copy-start(bf16[16,256,1024]{2,1,0:T(8,128)(2,1)} %x_ref.1) | copy-start | bytes 25165828
  0.0 481.8 %collective-permute-start = (bf16[16,64,1024]{2,1,0:T(8,128)(2,1)}, bf16[16,64,1024]{2,1,0:T(8,128)(2,1)}, u32[]{:S(2)}, u32[]{:S(2)}) collective-permute-start(bf16[16,64,1024]{2,1,0:T(8,128)(2,1)} %param.16), channel_id=1, source_target_pairs={{0,16},{1,17},{2,18},{3,19},{4,20},{5,21},{6,22},{7,23},{8,24},{9,... | collective-permute-start | bytes 6291464 | tf_op jit(solution)/shard_map/ppermute | solution.py:191
  643.1 47.9 %collective-permute-start.1 = (bf16[16,64,1024]{2,1,0:T(8,128)(2,1)}, bf16[16,64,1024]{2,1,0:T(8,128)(2,1)S(1)}, u32[]{:S(2)}, u32[]{:S(2)}) collective-permute-start(bf16[16,64,1024]{2,1,0:T(8,128)(2,1)} %shard_map.139), channel_id=1, source_target_pairs={{0,16},{1,17},{2,18},{3,19},{4,20},{5,21},{6,22},{7,23},{8,24},{9,... | collective-permute-start | bytes 6291464 | tf_op jit(solution)/shard_map/ppermute | solution.py:207

commit v2 on v1

--- a/solution.py
+++ b/solution.py
@@ -9,7 +9,7 @@
 from jax.sharding import PartitionSpec as P
 
 NEG = -1e30
-VMEM_LIMIT = 60 * 1024 * 1024
+VMEM_LIMIT = 67043328
 ENC_STEP = 2
 DEC_STEP = 4
 
@@ -54,7 +54,7 @@
     ]
 
 
-def enc_kernel(layer, chunk, len_ref, qkv_ref, x_ref, wo_hbm, w1_hbm, w2_hbm, out_ref, wo, w1, w2, mixed, state_s, hidden, sems):
+def enc_kernel(layer, chunk, begin, len_ref, qkv_ref, x_ref, wo_hbm, w1_hbm, w2_hbm, out_ref, norm_ref, wo, w1, w2, mixed, state_s, hidden, sems):
     step = pl.program_id(0)
     first = step == 0
     copies = weight_copies(layer, (wo_hbm, w1_hbm, w2_hbm), (wo, w1, w2), sems)
@@ -68,7 +68,7 @@
 
     def one(b, carry):
         rows = pl.ds(pl.multiple_of(b * length, length), length)
-        valid = lax.broadcasted_iota(jnp.int32, (1, length), 1) < len_ref[step * seqs + b]
+        valid = lax.broadcasted_iota(jnp.int32, (1, length), 1) < len_ref[(begin + step) * seqs + b]
         for h in range(heads):
             mixed[rows, h * head:(h + 1) * head] = attend(qkv_ref[b, 0, h], qkv_ref[b, 1, h], qkv_ref[b, 2, h], valid)
         return carry
@@ -87,10 +87,12 @@
         copies[1].wait()
         copies[2].wait()
 
-    out_ref[...] = ffn(state_s[...], w1, w2, hidden, chunk).reshape(out_ref.shape)
-
-
-def dec_kernel(layer, chunk, len_ref, qkv_ref, y_ref, kv_ref, wo_hbm, wq_hbm, cwo_hbm, w1_hbm, w2_hbm, out_ref,
+    result = ffn(state_s[...], w1, w2, hidden, chunk)
+    out_ref[...] = result.reshape(out_ref.shape)
+    norm_ref[...] = rms_norm(result).reshape(out_ref.shape)
+
+
+def dec_kernel(layer, chunk, begin, len_ref, qkv_ref, y_ref, kv_ref, wo_hbm, wq_hbm, cwo_hbm, w1_hbm, w2_hbm, out_ref, norm_ref,
                wo, wq, cwo, w1, w2, mixed, query_s, state_s, hidden, sems):
     step = pl.program_id(0)
     first = step == 0
@@ -122,14 +124,14 @@
     query_s[...] = dot(rms_norm(state_s[...]), wq[...]).astype(jnp.bfloat16)
 
     for b in range(seqs):
-        valid = lax.broadcasted_iota(jnp.int32, (1, keys_len), 1) < len_ref[step * seqs + b]
+        valid = lax.broadcasted_iota(jnp.int32, (1, keys_len), 1) < len_ref[(begin + step) * seqs + b]
         at = slice(b * length, (b + 1) * length)
         for g in range(groups):
             spans = [slice((g * rep + r) * head, (g * rep + r + 1) * head) for r in range(rep)]
             query = jnp.concatenate([query_s[at, span] for span in spans], axis=0)
-            result = attend(query, kv_ref[0, b, 0, g], kv_ref[0, b, 1, g], valid)
+            answer = attend(query, kv_ref[0, b, 0, g], kv_ref[0, b, 1, g], valid)
             for r, span in enumerate(spans):
-                mixed[at, span] = result[r * length:(r + 1) * length]
+                mixed[at, span] = answer[r * length:(r + 1) * length]
 
     @pl.when(first)
     def _():
@@ -137,16 +139,21 @@
             copy.wait()
 
     state_s[...] = (state_s[...].astype(jnp.float32) + dot(mixed[...], cwo[...])).astype(jnp.bfloat16)
-    out_ref[...] = ffn(state_s[...], w1, w2, hidden, chunk).reshape(out_ref.shape)
-
-
-def call(kernel, step_seqs, lens, qkv, state, others, weights, layer, flops):
+    result = ffn(state_s[...], w1, w2, hidden, chunk)
+    out_ref[...] = result.reshape(out_ref.shape)
+    norm_ref[...] = rms_norm(result).reshape(out_ref.shape)
+
+
+def call(kernel, step_seqs, lens, qkv, state, others, weights, layer, flops, begin=0, steps=None):
     n_seq, _, heads, length, head = qkv.shape
     d = state.shape[-1]
     width = weights[-1].shape[1]
     seqs = math.gcd(step_seqs, n_seq)
     rows = seqs * length
-    block = lambda *tail: pl.BlockSpec((seqs,) + tail, lambda i, lens: (i,) + (0,) * len(tail))
+    steps = n_seq // seqs if steps is None else steps
+    block = lambda *tail: pl.BlockSpec((seqs,) + tail, lambda i, lens: (begin + i,) + (0,) * len(tail))
+    result = pl.BlockSpec((seqs, length, d), lambda i, lens: (i, 0, 0))
+    out = jax.ShapeDtypeStruct((steps * seqs, length, d), state.dtype)
     scratch = [pltpu.VMEM(w.shape[1:], w.dtype) for w in weights]
     scratch.append(pltpu.VMEM((rows, heads * head), jnp.bfloat16))
     if others:
@@ -154,18 +161,18 @@
     scratch += [pltpu.VMEM((rows, d), jnp.bfloat16), pltpu.VMEM((rows, width), jnp.bfloat16)]
     scratch.append(pltpu.SemaphoreType.DMA((len(weights),)))
     other_specs = [
-        pl.BlockSpec((1, seqs) + o.shape[2:], lambda i, lens: (layer, i, 0, 0, 0, 0)) for o in others
+        pl.BlockSpec((1, seqs) + o.shape[2:], lambda i, lens: (layer, begin + i, 0, 0, 0, 0)) for o in others
     ]
     moved = 2 * sum(a.size for a in (qkv, state, state)) + sum(2 * w.size // w.shape[0] for w in weights)
     return pl.pallas_call(
-        functools.partial(kernel, layer, min(width, 1024)),
-        out_shape=jax.ShapeDtypeStruct(state.shape, state.dtype),
+        functools.partial(kernel, layer, min(width, 1024), begin),
+        out_shape=(out, out),
         grid_spec=pltpu.PrefetchScalarGridSpec(
             num_scalar_prefetch=1,
-            grid=(n_seq // seqs,),
+            grid=(steps,),
             in_specs=[block(3, heads, length, head), block(length, d)] + other_specs
             + [pl.BlockSpec(memory_space=pl.ANY)] * len(weights),
-            out_specs=block(length, d),
+            out_specs=(result, result),
             scratch_shapes=scratch,
         ),
         compiler_params=pltpu.CompilerParams(dimension_semantics=("arbitrary",), vmem_limit_bytes=VMEM_LIMIT),
@@ -173,8 +180,8 @@
     )(lens, qkv, state, *others, *weights)
 
 
-def project_qkv(state, w_qkv):
-    return jnp.einsum("bsd,dthe->bthse", rms_norm(state), w_qkv, preferred_element_type=jnp.float32).astype(jnp.bfloat16)
+def project_qkv(normed, w_qkv):
+    return jnp.einsum("bsd,dthe->bthse", normed, w_qkv, preferred_element_type=jnp.float32).astype(jnp.bfloat16)
 
 
 def merge_heads(w):
@@ -193,17 +200,27 @@
         enc_weights = [merge_heads(enc_wo), enc_w1, enc_w2]
         dec_weights = [merge_heads(dec_wo), cross_wq.reshape(cross_wq.shape[0], d, -1), merge_heads(cross_wo), dec_w1, dec_w2]
         macs = lambda ws: sum(w.size // w.shape[0] for w in ws)
-        state = x_enc
+        state, normed = x_enc, rms_norm(x_enc)
         for layer in range(enc_wqkv.shape[0]):
-            qkv = project_qkv(state, enc_wqkv[layer])
+            qkv = project_qkv(normed, enc_wqkv[layer])
             flops = 2 * state.size // d * (macs(enc_weights) + 2 * qkv.shape[2] * qkv.shape[4] * x_enc.shape[1])
-            state = call(enc_kernel, ENC_STEP, enc_len, qkv, state, [], enc_weights, layer, flops)
-        kv_all = jnp.einsum("bsd,ldtge->lbtgse", rms_norm(state), cross_wkv, preferred_element_type=jnp.float32).astype(jnp.bfloat16)
-        state = guest
-        for layer in range(dec_wqkv.shape[0]):
-            qkv = project_qkv(state, dec_wqkv[layer])
+            state, normed = call(enc_kernel, ENC_STEP, enc_len, qkv, state, [], enc_weights, layer, flops)
+        kv_all = jnp.einsum("bsd,ldtge->lbtgse", normed, cross_wkv, preferred_element_type=jnp.float32).astype(jnp.bfloat16)
+        state, normed = guest, rms_norm(guest)
+        last = dec_wqkv.shape[0] - 1
+        total = y.shape[0] // math.gcd(DEC_STEP, y.shape[0])
+        half, quarter = total - total // 2, total // 4
+        pieces = [(0, half), (half, total - half - quarter), (total - quarter, quarter)]
+        for layer in range(last + 1):
+            qkv = project_qkv(normed, dec_wqkv[layer])
             flops = 2 * state.size // d * (macs(dec_weights) + 4 * qkv.shape[2] * qkv.shape[4] * x_enc.shape[1])
-            state = call(dec_kernel, DEC_STEP, enc_len, qkv, state, [kv_all], dec_weights, layer, flops)
-        return lax.ppermute(state, "stage", swap)
+            run = functools.partial(call, dec_kernel, DEC_STEP, enc_len, qkv, state, [kv_all], dec_weights, layer)
+            if layer < last:
+                state, normed = run(flops)
+        sent = []
+        for begin, steps in pieces:
+            if steps:
+                sent.append(lax.ppermute(run(flops * steps // (64 * total), begin, steps)[0], "stage", swap))
+        return jnp.concatenate(sent, axis=0)
 
     return jax.shard_map(body, mesh=mesh, in_specs=(rows, rows, rows) + (whole,) * 11, out_specs=rows, check_vma=False)

time: 702 us -> 678 us (0.966)
  waiting for transfers between devices: 47.3 us -> 13.1 us
  Pallas kernels: 360 us -> 377 us
  other arithmetic: 16.1 us -> 6.74 us
    ppermute x1 -> x3, waiting for transfers between devices: 47.3 us -> 13.1 us  [body(): lax.ppermute(run(flops * steps // (64 * total), begin, steps)[0], 'stage'...]
    pallas_call x4 -> x6, Pallas kernels: 360 us -> 377 us  [call(): pl.pallas_call(functools.partial(kernel, layer, min(width, 1024), begin),...]
    reduce_sum x5 -> x2, other arithmetic: 16 us -> 3.77 us  [rms_norm(): jnp.mean(wide * wide, axis=-1, keepdims=True) + 1e-06]
  transfers between devices with their start and end apart: 2 -> 4, of which waited for: 1 -> 1; matrix products, arithmetic and copies ran while one was open for 33% -> 33% of each run, Pallas kernels for 35% -> 43%
where the time goes in v2:
time: 678 us; the launch traced here: 668 us
  Pallas kernels  377 us (56%)
  matrix products  210 us (31%)
  local copies, waits for them, and re-layouts  51.5 us (8%)
  waiting for transfers between devices  13.1 us (2%)
  starting transfers between devices  8.57 us (1%)
    pallas_call x6, Pallas kernels, call(): pl.pallas_call(functools.partial(kernel, layer, min(width, 1024), begin),...  377 us
    dot_general x4, matrix products, project_qkv(): jnp.einsum('bsd,dthe->bthse', normed, w_qkv, preferred_element_type=jnp.f...  167 us
    dot_general x1, matrix products, body(): jnp.einsum('bsd,ldtge->lbtgse', normed, cross_wkv, preferred_element_type...  43.5 us
    slice x1, local copies, waits for them, and re-layouts, body(): qkv = project_qkv(normed, enc_wqkv[layer])  18.6 us
    slice x1, local copies, waits for them, and re-layouts, body(): qkv = project_qkv(normed, dec_wqkv[layer])  18.5 us
    reshape x1, local copies, waits for them, and re-layouts, body(): cross_wq.reshape(cross_wq.shape[0], d, -1)  14.4 us
  transfers between devices with their start and end apart: 4, of which 1 were waited for; matrix products, arithmetic and copies ran while one was open for 33% of the time, Pallas kernels for 43%

profile of v2, /device:TPU:97, one launch (start us, length us, event | category | flops | bytes accessed | tf_op | source)
XLA Modules:
  0.0 667.9 jit_solution(13851214114972216912)
XLA Ops:
  0.0 4.8 collective-permute-start
  4.8 18.6 %fusion.17 = (bf16[1,1024,3,16,128]{4,3,2,1,0:T(8,128)(2,1)}, bf16[1024,3,16,128,1]{3,2,1,0,4:T(8,128)(2,1)}) fusion(bf16[2,1024,3,16,128]{4,3,2,1,0:T(8,128)(2,1)} %param.17), kind=kLoop, calls=%fused_computation.31 | loop fusion | bytes 50331648 | tf_op jit(solution)/shard_map/slice | solution.py:205
  23.4 1.7 fusion
  25.2 62.5 %convert_bitcast_fusion.1.qkv_ref = bf16[16,3,16,256,128]{4,3,2,1,0:T(8,128)(2,1)} fusion(bf16[1,1024,3,16,128]{4,3,2,1,0:T(8,128)(2,1)} %get-tuple-element.21, bf16[16,256,1024]{2,1,0:T(8,128)(2,1)} %x_ref.1, f32[16,256]{1,0:T(8,128)S(1)} %add_rsqrt_fusion), kind=kOutput, calls=%fused_computation.1 | convolution fusion | flops 51577356288 | bytes 71319552 | tf_op jit(solution)/shard_map/bsd,dthe->bthse/dot_general | solution.py:184
  87.7 125.2 %shard_map.136 = (bf16[16,256,1024]{2,1,0:T(8,128)(2,1)}, bf16[16,256,1024]{2,1,0:T(8,128)(2,1)}) custom-call(s32[16]{0:T(128)} %len_ref.11, bf16[16,3,16,256,128]{4,3,2,1,0:T(8,128)(2,1)} %convert_bitcast_fusion.1.qkv_ref, bf16[16,256,1024]{2,1,0:T(8,128)(2,1)} %x_ref.1, bf16[2,2048,1024]{2,1,0:T(8,128)(2,1)} %bitcast.70, bf16[2,1024,3072]{2,1,0:T(8,128)(2,1)} %w1_hbm.7, ...), custom_call_target="tpu_custom_call" | custom-call | flops 77309411328 | bytes 83886080 | tf_op jit(solution)/shard_map/pallas_call | solution.py:167
  212.9 61.4 %convert_bitcast_fusion.qkv_ref = bf16[16,3,16,256,128]{4,3,2,1,0:T(8,128)(2,1)} fusion(bf16[1024,3,16,128,1]{3,2,1,0,4:T(8,128)(2,1)} %get-tuple-element.22, bf16[16,256,1024]{2,1,0:T(8,128)(2,1)} %get-tuple-element.13), kind=kOutput, calls=%fused_computation | convolution fusion | flops 51564773376 | bytes 71303168 | tf_op jit(solution)/shard_map/bsd,dthe->bthse/dot_general | solution.py:184
  274.3 124.9 %shard_map.137 = (bf16[16,256,1024]{2,1,0:T(8,128)(2,1)}, bf16[16,256,1024]{2,1,0:T(8,128)(2,1)}) custom-call(s32[16]{0:T(128)} %len_ref.11, bf16[16,3,16,256,128]{4,3,2,1,0:T(8,128)(2,1)} %convert_bitcast_fusion.qkv_ref, bf16[16,256,1024]{2,1,0:T(8,128)(2,1)} %get-tuple-element.14.x_ref, bf16[2,2048,1024]{2,1,0:T(8,128)(2,1)} %bitcast.71, ...), custom_call_target="tpu_custom_call" | custom-call | flops 77309411328 | bytes 83886080 | tf_op jit(solution)/shard_map/pallas_call | solution.py:167
  399.2 43.5 %convert_bitcast_fusion.2.kv_ref = bf16[2,16,2,8,256,128]{5,4,3,2,1,0:T(8,128)(2,1)} fusion(bf16[16,256,1024]{2,1,0:T(8,128)(2,1)} %get-tuple-element.15, bf16[2,1024,2,8,128,1]{4,3,2,1,0,5:T(8,128)(2,1)} %bitcast.72), kind=kOutput, calls=%fused_computation.2 | convolution fusion | flops 34376515584 | bytes 50331648 | tf_op jit(solution)/shard_map/bsd,ldtge->lbtgse/dot_general | solution.py:208
  442.7 14.4 %reshape.30.wq_hbm = bf16[2,1024,2048]{2,1,0:T(8,128)(2,1)} reshape(bf16[2,1024,8,2,128]{4,3,2,1,0:T(2,128)(2,1)} %param.23) | data formatting | bytes 16777216 | tf_op jit(solution)/shard_map/reshape | solution.py:201
  457.1 18.5 %fusion.18 = (bf16[1,1024,3,16,128]{4,3,2,1,0:T(8,128)(2,1)}, bf16[1,1024,3,16,128]{4,3,2,1,0:T(8,128)(2,1)}) fusion(bf16[2,1024,3,16,128]{4,3,2,1,0:T(8,128)(2,1)} %param.21), kind=kLoop, calls=%fused_computation.32 | loop fusion | bytes 50331648 | tf_op jit(solution)/shard_map/slice | solution.py:215
  475.6 0.0 collective-permute-done.y_ref
  475.6 2.1 fusion.11
  477.7 21.3 %convert_bitcast_fusion.4.qkv_ref = bf16[16,3,16,64,128]{4,3,2,1,0:T(8,128)(2,1)} fusion(bf16[1,1024,3,16,128]{4,3,2,1,0:T(8,128)(2,1)} %get-tuple-element.23, bf16[16,64,1024]{2,1,0:T(8,128)(2,1)} %collective-permute-done.y_ref, f32[16,64]{1,0:T(8,128)S(1)} %add_rsqrt_fusion.1), kind=kOutput, calls=%fused_computation.15 | convolution fusion | flops 12894339072 | bytes 27267072 | tf_op jit(solution)/shard_map/bsd,dthe->bthse/dot_general | solution.py:184
  499.0 58.0 %shard_map.138 = (bf16[16,64,1024]{2,1,0:T(8,128)(2,1)}, bf16[16,64,1024]{2,1,0:T(8,128)(2,1)}) custom-call(s32[16]{0:T(128)} %len_ref.11, bf16[16,3,16,64,128]{4,3,2,1,0:T(8,128)(2,1)} %convert_bitcast_fusion.4.qkv_ref, bf16[16,64,1024]{2,1,0:T(8,128)(2,1)} %collective-permute-done.y_ref, bf16[2,16,2,8,256,128]{5,4,3,2,1,0:T(8,128)(2,1)} %convert_bitcast_fusion.2.kv_ref, ...), custom_call_target="tpu_custom_call" | custom-call | flops 30064771072 | bytes 41943040 | tf_op jit(solution)/shard_map/pallas_call | solution.py:167
  557.0 21.6 %convert_bitcast_fusion.3.qkv_ref = bf16[16,3,16,64,128]{4,3,2,1,0:T(8,128)(2,1)} fusion(bf16[1,1024,3,16,128]{4,3,2,1,0:T(8,128)(2,1)} %get-tuple-element.24, bf16[16,64,1024]{2,1,0:T(8,128)(2,1)} %get-tuple-element.16), kind=kOutput, calls=%fused_computation.13 | convolution fusion | flops 12891193344 | bytes 27262976 | tf_op jit(solution)/shard_map/bsd,dthe->bthse/dot_general | solution.py:184
  578.6 32.5 %shard_map.139 = (bf16[8,64,1024]{2,1,0:T(8,128)(2,1)}, bf16[8,64,1024]{2,1,0:T(8,128)(2,1)}) custom-call(s32[16]{0:T(128)} %len_ref.11, bf16[16,3,16,64,128]{4,3,2,1,0:T(8,128)(2,1)} %convert_bitcast_fusion.3.qkv_ref, bf16[16,64,1024]{2,1,0:T(8,128)(2,1)} %get-tuple-element.17.y_ref, bf16[2,16,2,8,256,128]{5,4,3,2,1,0:T(8,128)(2,1)} %convert_bitcast_fusion.2.kv_ref, ...), custom_call_target="tpu_custom_call" | custom-call | flops 234881024 | bytes 41943040 | tf_op jit(solution)/shard_map/pallas_call | solution.py:167
  611.1 0.6 collective-permute-start.1
  611.7 18.4 %shard_map.140 = (bf16[4,64,1024]{2,1,0:T(8,128)(2,1)}, bf16[4,64,1024]{2,1,0:T(8,128)(2,1)}) custom-call(s32[16]{0:T(128)} %len_ref.11, bf16[16,3,16,64,128]{4,3,2,1,0:T(8,128)(2,1)} %convert_bitcast_fusion.3.qkv_ref, bf16[16,64,1024]{2,1,0:T(8,128)(2,1)} %get-tuple-element.17.y_ref, bf16[2,16,2,8,256,128]{5,4,3,2,1,0:T(8,128)(2,1)} %convert_bitcast_fusion.2.kv_ref, ...), custom_call_target="tpu_custom_call" | custom-call | flops 117440512 | bytes 41943040 | tf_op jit(solution)/shard_map/pallas_call | solution.py:167
  630.1 2.6 collective-permute-start.2
  632.7 18.4 %shard_map.141 = (bf16[4,64,1024]{2,1,0:T(8,128)(2,1)}, bf16[4,64,1024]{2,1,0:T(8,128)(2,1)}) custom-call(s32[16]{0:T(128)} %len_ref.11, bf16[16,3,16,64,128]{4,3,2,1,0:T(8,128)(2,1)} %convert_bitcast_fusion.3.qkv_ref, bf16[16,64,1024]{2,1,0:T(8,128)(2,1)} %get-tuple-element.17.y_ref, bf16[2,16,2,8,256,128]{5,4,3,2,1,0:T(8,128)(2,1)} %convert_bitcast_fusion.2.kv_ref, ...), custom_call_target="tpu_custom_call" | custom-call | flops 117440512 | bytes 41943040 | tf_op jit(solution)/shard_map/pallas_call | solution.py:167
  651.0 0.6 collective-permute-start.3
  651.6 13.0 %collective-permute-done.3 = bf16[4,64,1024]{2,1,0:T(8,128)(2,1)S(1)} collective-permute-done((bf16[4,64,1024]{2,1,0:T(8,128)(2,1)}, bf16[4,64,1024]{2,1,0:T(8,128)(2,1)S(1)}, u32[]{:S(2)}, u32[]{:S(2)}) %collective-permute-start.3) | collective-permute-done | bytes 524320 | tf_op jit(solution)/shard_map/ppermute | solution.py:223
  664.7 0.0 collective-permute-done.1
  664.7 2.9 pad_maximum_fusion
  (5 shorter events, 0.0 us)
Async XLA Ops:
  0.0 23.4 %copy-start = (bf16[16,256,1024]{2,1,0:T(8,128)(2,1)S(1)}, bf16[16,256,1024]{2,1,0:T(8,128)(2,1)}, u32[]{:S(2)}) copy-start(bf16[16,256,1024]{2,1,0:T(8,128)(2,1)} %x_ref.1) | copy-start | bytes 25165828
  0.0 475.6 %collective-permute-start = (bf16[16,64,1024]{2,1,0:T(8,128)(2,1)}, bf16[16,64,1024]{2,1,0:T(8,128)(2,1)}, u32[]{:S(2)}, u32[]{:S(2)}) collective-permute-start(bf16[16,64,1024]{2,1,0:T(8,128)(2,1)} %param.16), channel_id=1, source_target_pairs={{0,16},{1,17},{2,18},{3,19},{4,20},{5,21},{6,22},{7,23},{8,24},{9,... | collective-permute-start | bytes 6291464 | tf_op jit(solution)/shard_map/ppermute | solution.py:198
  611.1 53.6 %collective-permute-start.1 = (bf16[8,64,1024]{2,1,0:T(8,128)(2,1)}, bf16[8,64,1024]{2,1,0:T(8,128)(2,1)}, u32[]{:S(2)}, u32[]{:S(2)}) collective-permute-start(bf16[8,64,1024]{2,1,0:T(8,128)(2,1)} %get-tuple-element.18), channel_id=1, source_target_pairs={{0,16},{1,17},{2,18},{3,19},{4,20},{5,21},{6,22},{7,23},{8,24},{9,... | collective-permute-start | bytes 3145736 | tf_op jit(solution)/shard_map/ppermute | solution.py:223
  630.1 21.6 %collective-permute-start.2 = (bf16[4,64,1024]{2,1,0:T(8,128)(2,1)}, bf16[4,64,1024]{2,1,0:T(8,128)(2,1)}, u32[]{:S(2)}, u32[]{:S(2)}) collective-permute-start(bf16[4,64,1024]{2,1,0:T(8,128)(2,1)} %get-tuple-element.19), channel_id=1, source_target_pairs={{0,16},{1,17},{2,18},{3,19},{4,20},{5,21},{6,22},{7,23},{8,24},{9,... | collective-permute-start | bytes 1572872 | tf_op jit(solution)/shard_map/ppermute | solution.py:223
  651.0 13.6 %collective-permute-start.3 = (bf16[4,64,1024]{2,1,0:T(8,128)(2,1)}, bf16[4,64,1024]{2,1,0:T(8,128)(2,1)S(1)}, u32[]{:S(2)}, u32[]{:S(2)}) collective-permute-start(bf16[4,64,1024]{2,1,0:T(8,128)(2,1)} %get-tuple-element.20), channel_id=1, source_target_pairs={{0,16},{1,17},{2,18},{3,19},{4,20},{5,21},{6,22},{7,23},{8,24},{9,... | collective-permute-start | bytes 1572872 | tf_op jit(solution)/shard_map/ppermute | solution.py:223
